TPU v7x, 32 devices: a whole 2x2x4 slice. The times are simulated.
32 devices in a mesh: wide: 8 (over y, x, core), narrow: 4 (over z).
Axes of the slice: x: 2, y: 2, z: 4, core: 2. Of those that a mesh axis runs over, the one named last changes fastest.
Arguments:
- momentum: float32 [9216, 9216], P('wide', 'narrow'), may hold values from -3 to 3
- gradient: bfloat16 [9216, 9216], P('wide', 'narrow'), may hold values from -48 to 48
- right_factor: float32 [512, 9216], P('wide', 'narrow'), may hold values from -6 to 6
Outputs:
- new_momentum: float32 [9216, 9216], P('wide', 'narrow')
- new_right: float32 [512, 9216], P('wide', 'narrow')
- update: bfloat16 [9216, 9216], P('wide', 'narrow')
All inputs are finite; a program needn't handle non-finite values.
Results may differ from a plain program's by a relative error of at most 0.001.
Values sent between devices are 32-bit elements; how exact they have to be, the bound alone decides.
No kernel may reach another device: no remote copies, remote signals or barrier semaphores. Data moves between devices by JAX's collectives and lax.ppermute only.
A program may use at most 128 MiB of HBM per device.

v0:
```python
import jax
import jax.numpy as jnp
from jax import lax
from jax.sharding import PartitionSpec as P

N_COLS = 9216


EPS = 1e-06
MU = 0.95


def orthonormal(projected, gram_matrix):
    factor_lower = jnp.linalg.cholesky(gram_matrix)
    return jax.scipy.linalg.solve_triangular(factor_lower, projected.T, lower=True).T


def matmul(left, right):
    return jnp.dot(left, right, preferred_element_type=jnp.float32, precision=lax.Precision.HIGHEST)


def per_device(momentum, gradient, right_factor):
    blended = momentum + gradient.astype(jnp.float32)
    partial_left = matmul(blended, lax.all_gather(right_factor, "wide", axis=0, tiled=True).T)
    projected = lax.psum(partial_left, "narrow")
    gram_matrix = lax.psum(matmul(projected.T, projected), "wide")
    left_basis = orthonormal(projected, gram_matrix)
    columns = left_basis
    right_block = lax.psum_scatter(
        matmul(columns.T, blended), "wide", scatter_dimension=0, tiled=True
    )
    squares = lax.psum(jnp.sum(right_block * right_block, axis=1), "narrow")
    root_mean = jnp.sqrt(squares / N_COLS + EPS)
    new_right = right_block / root_mean[:, None]
    pieces = (
        lax.all_gather(right_block, "wide", axis=0, tiled=True),
        lax.all_gather(root_mean, "wide", axis=0, tiled=True),
    )
    columns = left_basis
    normed = pieces[0] / pieces[1][:, None]
    feedback = matmul(columns, pieces[0])
    direction = matmul(columns, normed)
    new_momentum = blended - (1.0 - MU) * feedback
    return (new_momentum, new_right, direction.astype(jnp.bfloat16))


def solution(mesh):
    return jax.shard_map(
        per_device,
        mesh=mesh,
        in_specs=(P("wide", "narrow"), P("wide", "narrow"), P("wide", "narrow")),
        out_specs=(P("wide", "narrow"), P("wide", "narrow"), P("wide", "narrow")),
        check_vma=False,
    )
```

profile of v0, /device:TPU:0, one launch (start us, length us, event | category | flops | bytes accessed | tf_op | source)
XLA Modules:
  0.0 566.0 jit_solution(15770033689719844626)
XLA Ops:
  7.2 0.7 all-gather.3.cloned.1.call-update
  7.9 43.5 %all-gather.3.cloned.1.call-done = f32[512,2304]{1,0:T(8,128)} async-done(((f32[64,2304]{1,0:T(8,128)}), f32[512,2304]{1,0:T(8,128)}) %all-gather.3.cloned.1.call-update) | async-done | bytes 4718608 | tf_op jit(solution)/shard_map/all_gather | solution.py:24
  51.4 22.9 %fusion.3 = f32[1152,512]{1,0:T(8,128)} fusion(f32[512,2304]{1,0:T(8,128)} %all-gather.3.cloned.1.call-done, f32[1152,2304]{1,0:T(8,128)} %param.3, bf16[1152,2304]{1,0:T(8,128)(2,1)} %param.4), kind=kOutput, calls=%fused_computation.8 | convolution fusion | flops 16312762368 | bytes 23003136 | tf_op jit(solution)/shard_map/dot_general | solution.py:19
  74.4 94.7 %all-reduce.5.cloned.1.call-done = f32[1152,512]{1,0:T(8,128)} async-done(((f32[1152,512]{1,0:T(8,128)}), f32[1152,512]{1,0:T(8,128)}) %all-reduce.5.cloned.1.call-update) | async-done | bytes 2359312 | tf_op jit(solution)/shard_map/psum | solution.py:25
  169.1 7.7 %fusion.40 = f32[512,512]{0,1:T(8,128)} fusion(f32[1152,512]{1,0:T(8,128)} %all-reduce.5.cloned.1.call-done), kind=kOutput, calls=%fused_computation.82 | convolution fusion | flops 3623878656 | bytes 3407872 | tf_op jit(solution)/shard_map/dot_general | solution.py:19
  177.1 55.6 %all-reduce.7.cloned.1.call-done = f32[512,512]{0,1:T(8,128)} async-done(((f32[512,512]{0,1:T(8,128)}), f32[512,512]{0,1:T(8,128)}) %all-reduce.7.cloned.1.call-update) | async-done | bytes 1048592 | tf_op jit(solution)/shard_map/psum | solution.py:26
  232.7 1.6 copy.7
  234.6 1.0 copy-done.5
  235.6 11.7 %cholesky.104 = f32[128,128]{1,0:T(8,128)S(1)} custom-call(f32[128,128]{1,0:T(8,128)S(1)} %cholesky.266), custom_call_target="Cholesky" | custom-call | tf_op jit(solution)/shard_map/jit(cholesky)/cholesky | solution.py:14
  247.3 9.8 %custom-call.31 = f32[1,128,128]{1,2,0:T(8,128)S(1)} custom-call(f32[1,128,128]{2,1,0:T(8,128)S(1)} %get-tuple-element.30), custom_call_target="InvertDiagBlocksLowerTriangular" | custom-call | tf_op jit(solution)/shard_map/jit(cholesky)/cholesky | solution.py:14
  257.2 1.2 constant_dynamic-update-slice_fusion.3
  258.5 1.3 convolution_subtract_fusion.3
  259.8 11.7 %cholesky.217 = f32[128,128]{1,0:T(8,128)S(1)} custom-call(f32[128,128]{1,0:T(8,128)S(1)} %cholesky.270), custom_call_target="Cholesky" | custom-call | tf_op jit(solution)/shard_map/jit(cholesky)/cholesky | solution.py:14
  271.5 10.2 %custom-call.32 = f32[1,128,128]{1,2,0:T(8,128)S(1)} custom-call(f32[1,128,128]{2,1,0:T(8,128)S(1)} %get-tuple-element.27), custom_call_target="InvertDiagBlocksLowerTriangular" | custom-call | tf_op jit(solution)/shard_map/jit(cholesky)/cholesky | solution.py:14
  282.0 1.4 convolution_subtract_fusion.4
  283.4 0.6 cholesky.275
  284.1 13.2 %cholesky.238 = f32[128,128]{1,0:T(8,128)} custom-call(f32[128,128]{1,0:T(8,128)} %cholesky.275), custom_call_target="Cholesky" | custom-call | tf_op jit(solution)/shard_map/jit(cholesky)/cholesky | solution.py:14
  297.2 1.5 select_reduce_fusion.1
  298.7 0.7 compare_reduce_fusion.1
  299.4 11.3 %custom-call.33 = f32[1,128,128]{1,2,0:T(8,128)} custom-call(f32[1,128,128]{2,1,0:T(8,128)} %get-tuple-element.24), custom_call_target="InvertDiagBlocksLowerTriangular" | custom-call | tf_op jit(solution)/shard_map/jit(cholesky)/cholesky | solution.py:14
  310.7 1.0 convolution_dynamic-update-slice_fusion.1
  311.8 1.2 convolution_subtract_fusion.5
  313.0 11.7 %cholesky.255 = f32[128,128]{1,0:T(8,128)S(1)} custom-call(f32[128,128]{1,0:T(8,128)S(1)} %convolution_subtract_fusion.5), custom_call_target="Cholesky" | custom-call | tf_op jit(solution)/shard_map/jit(cholesky)/cholesky | solution.py:14
  324.7 0.6 compare_reduce_fusion
  325.4 0.6 compare_reduce_fusion.2
  328.5 1.3 select_select_fusion
  329.8 13.7 %while.1 = (s32[]{:T(128)}, f32[512,512]{1,0:T(8,128)}, s32[4,2]{0,1:T(2,128)S(1)}, f32[4,128,128]{2,1,0:T(8,128)}, s32[]{:T(128)}) while((s32[]{:T(128)}, f32[512,512]{1,0:T(8,128)}, s32[4,2]{0,1:T(2,128)S(1)}, f32[4,128,128]{2,1,0:T(8,128)}, s32[]{:T(128)}) %tuple.32), condition=%wide.while_cond, body=%wide.while_body.sunk | while | flops 2 | bytes 132205 | solution.py:15
  330.4 2.8 bitcast_dynamic-update-slice_fusion.2
  333.8 2.8 bitcast_dynamic-update-slice_fusion.2
  337.3 2.8 bitcast_dynamic-update-slice_fusion.2
  340.7 2.8 bitcast_dynamic-update-slice_fusion.2
  343.5 40.1 %custom-call.34 = f32[4,128,128]{1,2,0:T(8,128)S(1)} custom-call(f32[4,128,128]{2,1,0:T(8,128)} %get-tuple-element.10), custom_call_target="InvertDiagBlocksLowerTriangular" | custom-call | tf_op jit(solution)/shard_map/jit(_solve_triangular)/triangular_solve | solution.py:15
  383.6 0.7 fusion.14
  384.4 2.4 convolution_subtract_fusion.2
  386.8 1.6 fusion.27
  388.4 3.0 convolution_subtract_fusion.1
  391.5 0.7 fusion.25
  392.2 4.2 convolution_subtract_fusion
  396.5 0.7 fusion.24
  397.3 23.1 %fusion.2 = f32[512,2304]{1,0:T(8,128)} fusion(f32[1152,2304]{1,0:T(8,128)} %param.3, bf16[1152,2304]{1,0:T(8,128)(2,1)S(1)} %bitcast.55, f32[128,1152]{1,0:T(8,128)S(1)} %fusion.24, f32[128,1152]{1,0:T(8,128)S(1)} %fusion.25, f32[128,1152]{1,0:T(8,128)S(1)} %fusion.27, f32[128,1152]{1,0:T(8,128)S(1)} %fusion.14), kind=kOutput, calls=%fused_computation.7 | convolution fusion | flops 16314531840 | bytes 23003136 | tf_op jit(solution)/shard_map/dot_general | solution.py:19
  420.4 53.1 %reduce-scatter.2.cloned.1.call-done = f32[64,2304]{1,0:T(8,128)} async-done(((f32[512,2304]{1,0:T(8,128)}), f32[64,2304]{1,0:T(8,128)}) %reduce-scatter.2.cloned.1.call-update) | async-done | bytes 589840 | tf_op jit(solution)/shard_map/reduce_scatter | solution.py:29
  474.8 1.2 multiply_reduce_fusion
  476.0 11.7 %psum.23 = f32[64]{0:T(128)S(1)} all-reduce(f32[64]{0:T(128)S(1)} %multiply_reduce_fusion), channel_id=1, replica_groups=mesh['wide'=8,'narrow'=4] {'narrow'}, use_global_device_ids=true, to_apply=%region_12.13 | all-reduce | flops 64 | bytes 512 | tf_op jit(solution)/shard_map/psum | solution.py:32
  487.8 12.1 %all-reduce.1 = f32[512]{0:T(512)S(1)} all-reduce(f32[512]{0:T(512)S(1)} %get-tuple-element.31), channel_id=1, replica_groups=mesh['wide'=8,'narrow'=4] {'wide'}, use_global_device_ids=true, to_apply=%add.1 | all-reduce | flops 512 | bytes 4096
  499.9 2.0 broadcast_divide_fusion
  501.9 12.3 %all-gather.5.cloned.1.call-done = f32[512,2304]{1,0:T(8,128)} async-done(((f32[64,2304]{1,0:T(8,128)}), f32[512,2304]{1,0:T(8,128)}) %all-gather.5.cloned.1.call-update) | async-done | bytes 4718608 | tf_op jit(solution)/shard_map/all_gather | solution.py:36
  514.2 24.1 %fusion = f32[1152,2304]{1,0:T(8,128)} fusion(f32[512,2304]{1,0:T(8,128)} %all-gather.5.cloned.1.call-done, f32[1152,2304]{1,0:T(8,128)} %param.3, bf16[1152,2304]{1,0:T(8,128)(2,1)} %param.4, f32[128,1152]{1,0:T(8,128)S(1)} %fusion.24, f32[128,1152]{1,0:T(8,128)S(1)} %copy-done.2, f32[128,1152]{1,0:T(8,128)S(1)} %fusion.27, f32[128,1152]{1,0:T(8,128)S(1)} %fusion.14), kind=kOutput, calls=%fused_computation.3 | convolution fusion | flops 16319840256 | bytes 33619968 | tf_op jit(solution)/shard_map/dot_general | solution.py:19
  538.3 20.7 %convolution_convert_fusion = bf16[1152,2304]{1,0:T(8,128)(2,1)} fusion(f32[512,2304]{1,0:T(8,128)S(1)} %copy-done.3, f32[512]{0:T(512)S(1)} %all-reduce.1, f32[128,1152]{1,0:T(8,128)S(1)} %fusion.24, f32[128,1152]{1,0:T(8,128)S(1)} %copy-done.2, f32[128,1152]{1,0:T(8,128)S(1)} %fusion.27, f32[128,1152]{1,0:T(8,128)S(1)} %fusion.14), kind=kOutput, calls=%fused_computation.4 | convolution fusion | flops 16313057280 | bytes 12388352 | tf_op jit(solution)/shard_map/dot_general | solution.py:19
  (53 shorter events, 4.3 us)
Async XLA Ops:
  7.2 44.2 %all-gather.3.cloned.1.call-start = ((), (), s32[]{:S(2)}) async-start(), calls=%async_computation.1 | async-start | bytes 5308416 | tf_op jit(solution)/shard_map/all_gather | solution.py:24
  7.9 161.2 %all-reduce.5.cloned.1.call-start = ((), (), s32[]{:S(2)}) async-start(), calls=%async_computation.2 | async-start | bytes 4718592 | tf_op jit(solution)/shard_map/psum | solution.py:25
  74.3 158.4 %all-reduce.7.cloned.1.call-start = ((), (), s32[]{:S(2)}) async-start(), calls=%async_computation.3 | async-start | bytes 2097152 | tf_op jit(solution)/shard_map/psum | solution.py:26
  176.8 296.7 %reduce-scatter.2.cloned.1.call-start = ((), (), s32[]{:S(2)}) async-start(), calls=%async_computation.4 | async-start | bytes 5308416 | tf_op jit(solution)/shard_map/reduce_scatter | solution.py:29
  232.7 1.7 copy-start.4
  234.6 1.0 copy-start.5
  282.0 101.6 %copy-start = (f32[1152,512]{1,0:T(8,128)S(1)}, f32[1152,512]{1,0:T(8,128)}, u32[]{:S(2)}) copy-start(f32[1152,512]{1,0:T(8,128)} %all-reduce.5.cloned.1.call-done) | copy-start | bytes 7077892
  383.6 0.8 copy-start.6
  383.6 13.6 %slice-start = ((s8[5308416]{0:T(1024)(128)(4,1)}), s8[4194304]{0:T(1024)(128)(4,1)S(1)}, s32[]{:S(2)}) async-start(s8[5308416]{0:T(1024)(128)(4,1)} %bitcast.54), calls=%async_computation.6 | async-start | bytes 8388608
  386.8 4.7 copy-start.7
  388.4 8.8 %slice-start.1 = ((s8[5308416]{0:T(1024)(128)(4,1)}), s8[1114112]{0:T(1024)(128)(4,1)S(1)}, s32[]{:S(2)}) async-start(s8[5308416]{0:T(1024)(128)(4,1)} %bitcast.54), calls=%async_computation.7 | async-start | bytes 2228224
  392.2 5.0 copy-start.1
  420.3 53.2 %copy-start.8 = (u32[32]{0:T(128)S(1)}, u32[32]{0:T(128)}, u32[]{:S(2)}) copy-start(u32[32]{0:T(128)} %constant.172) | copy-start | bytes 388
  420.4 93.8 %copy-start.2 = (f32[128,1152]{1,0:T(8,128)S(1)}, f32[128,1152]{1,0:T(8,128)}, u32[]{:S(2)}) copy-start(f32[128,1152]{1,0:T(8,128)} %copy-done.1) | copy-start | bytes 1769476
  420.4 93.8 %all-gather.5.cloned.1.call-start = ((), (), s32[]{:S(2)}) async-start(), calls=%async_computation.5 | async-start | bytes 5308416 | tf_op jit(solution)/shard_map/all_gather | solution.py:36
  514.2 24.1 %copy-start.3 = (f32[512,2304]{1,0:T(8,128)S(1)}, f32[512,2304]{1,0:T(8,128)}, u32[]{:S(2)}) copy-start(f32[512,2304]{1,0:T(8,128)} %all-gather.5.cloned.1.call-done) | copy-start | bytes 14155780
Sparse Core Ops, SparseCore 0:
  9.9 41.4 all-gather.2
  74.4 94.6 all-reduce.4
  176.9 55.7 all-reduce.6
  420.5 53.0 reduce-scatter.1
  475.3 38.9 all-gather.4
where the time goes:
time: 574 us; the launch traced here: 566 us
  waiting for transfers between devices  260 us (45%)
  other arithmetic  128 us (22%)
  matrix products  118 us (21%)
  blocking collectives  23.8 us (4%)
  between operations  17.8 us (3%)
  local copies, waits for them, and re-layouts  17.7 us (3%)
    dot_general x5, matrix products, matmul(): jnp.dot(left, right, preferred_element_type=jnp.float32, precision=lax.Pr...  98.4 us
    psum x1, waiting for transfers between devices, per_device(): projected = lax.psum(partial_left, 'narrow')  94.7 us
    another operation x14, other arithmetic, orthonormal(): factor_lower = jnp.linalg.cholesky(gram_matrix)  83.1 us
    psum x1, waiting for transfers between devices, per_device(): gram_matrix = lax.psum(matmul(projected.T, projected), 'wide')  55.6 us
    reduce_scatter x1, waiting for transfers between devices, per_device(): lax.psum_scatter(matmul(columns.T, blended), 'wide', scatter_dimension=0,...  53.1 us
    all_gather x1, waiting for transfers between devices, per_device(): lax.all_gather(right_factor, 'wide', axis=0, tiled=True)  43.5 us
    another operation x3, other arithmetic, orthonormal(): jax.scipy.linalg.solve_triangular(factor_lower, projected.T, lower=True)  41.4 us
    another operation x12, local copies, waits for them, and re-layouts  13.7 us
  transfers between devices with their start and end apart: 5, of which 5 were waited for; matrix products, arithmetic and copies ran while one was open for 1% of the time, Pallas kernels for 0%

commit v1 on v0

v1 whole, which is shorter than its diff:
```python
import jax
import jax.numpy as jnp
from jax import lax
from jax.experimental import pallas as pl
from jax.experimental.pallas import tpu as pltpu
from jax.sharding import PartitionSpec as P

EPS = 1e-06
MU = 0.95
HIGHEST = lax.Precision.HIGHEST
HIGH = lax.Precision.HIGH

def across(block, column):
    return jnp.broadcast_to(block[:, column:column + 1], block.shape)

def down(block, row):
    return jnp.broadcast_to(block[row:row + 1, :], block.shape)

def factor_block(rows):
    size = len(rows)
    lane = lax.broadcasted_iota(jnp.int32, (8, 128), 1)
    sub = lax.broadcasted_iota(jnp.int32, (8, 128), 0)
    for p in range(size):
        first = 8 * p
        panel = (lane >= first) & (lane < first + 8)
        cols = [across(rows[p], first + j) for j in range(8)]
        near = [across(rows[p + 1], first + j) for j in range(8)] if p + 1 < size else None
        low, scale = {}, []
        for j in range(8):
            scale.append(lax.rsqrt(down(cols[j], j)))
            cols[j] = cols[j] * scale[j]
            for t in range(j + 1, 8):
                low[t, j] = down(cols[j], t)
                cols[t] = cols[t] - cols[j] * low[t, j]
        start = jnp.where(panel, jnp.where(lane - first == sub, 1.0, 0.0), rows[p])
        done = []
        for j in range(8):
            x = down(start, j)
            for i in range(j):
                x = x - low[j, i] * done[i]
            done.append(x * scale[j])
        if near is not None:
            for j in range(8):
                near[j] = near[j] * scale[j]
                for t in range(j + 1, 8):
                    near[t] = near[t] - near[j] * low[t, j]
            x = jnp.where(panel, 0.0, rows[p + 1])
            rows[p + 1] = x - ((near[0] * done[0] + near[1] * done[1]) + (near[2] * done[2] + near[3] * done[3])
                               + ((near[4] * done[4] + near[5] * done[5]) + (near[6] * done[6] + near[7] * done[7])))
        if p + 2 < size:
            back = [None] * 8
            for j in reversed(range(8)):
                x = done[j]
                for i in range(j + 1, 8):
                    x = x - low[i, j] * back[i]
                back[j] = x * scale[j]
            for q in range(p + 2, size):
                x = jnp.where(panel, 0.0, rows[q])
                for j in range(8):
                    x = x - across(rows[q], first + j) * back[j]
                rows[q] = x
        x = done[0]
        for j in range(1, 8):
            x = jnp.where(sub == j, done[j], x)
        rows[p] = x
    return [jnp.where(lane <= 8 * p + sub, rows[p], 0.0) for p in range(size)]

def factor_kernel(gram_ref, out_ref):
    n = gram_ref.shape[0]
    nb = n // 128
    out_ref[...] = gram_ref[...]
    for kb in range(nb):
        ks, ke = kb * 128, kb * 128 + 128
        rows = [out_ref[ks + 8 * q:ks + 8 * q + 8, ks:ke] for q in range(16)]
        inv = jnp.concatenate(factor_block(rows), axis=0)
        if nb > 1:
            parts = []
            if kb > 0:
                parts.append(out_ref[ks:ke, :ks])
            if ke < n:
                parts.append(out_ref[ks:ke, ke:])
            other = jnp.concatenate(parts, axis=1) if len(parts) > 1 else parts[0]
            other = jnp.dot(inv, other, preferred_element_type=jnp.float32, precision=lax.Precision.HIGHEST)
            if kb > 0:
                out_ref[ks:ke, :ks] = other[:, :ks]
        if ke < n:
            upper = other[:, ks:]
            prods = [other[:, :ks]] if kb > 0 else []
            full = jnp.concatenate(prods + [inv, upper], axis=1)
            delta = lax.dot_general(upper, full, (((0,), (0,)), ((), ())), preferred_element_type=jnp.float32, precision=lax.Precision.HIGHEST)
            if kb > 0:
                out_ref[ke:, :ks] = out_ref[ke:, :ks] - delta[:, :ks]
            out_ref[ke:, ks:ke] = -delta[:, ks:ke]
            out_ref[ke:, ke:] = out_ref[ke:, ke:] - delta[:, ke:]
            out_ref[ks:ke, ke:] = jnp.zeros((128, n - ke), jnp.float32)
        out_ref[ks:ke, ks:ke] = inv

def inverse_factor(gram):
    return pl.pallas_call(factor_kernel, out_shape=jax.ShapeDtypeStruct(gram.shape, jnp.float32),
        name="inverse_factor",
        cost_estimate=pl.CostEstimate(flops=2*gram.shape[0]**3*32, bytes_accessed=8*gram.size, transcendentals=gram.shape[0]))(gram)


def contract(left, right, dims, precision):
    return lax.dot_general(left, right, (dims, ((), ())), preferred_element_type=jnp.float32, precision=precision)


def exchange_sum(x, axis, bit):
    size = lax.axis_size(axis)
    return x + lax.ppermute(x, axis, [(i, i ^ bit) for i in range(size)])


def bits_of(axis):
    size = lax.axis_size(axis)
    return [1 << b for b in range(size.bit_length() - 1)]


def sum_over(x, axis):
    size = lax.axis_size(axis)
    if size & (size - 1):
        return lax.psum(x, axis)
    bits = bits_of(axis)
    if x.shape[0] < 256:
        for bit in bits:
            x = exchange_sum(x, axis, bit)
        return x
    x = exchange_sum(x, axis, bits[0])
    half = x.shape[0] // 2
    first, second = x[:half], x[half:]
    rest = bits[1:]
    for bit, other in zip(rest, rest[::-1]):
        first, second = exchange_sum(first, axis, bit), exchange_sum(second, axis, other)
    return jnp.concatenate([first, second], axis=0)


def per_device(momentum, gradient, right_factor):
    columns = momentum.shape[1] * lax.axis_size("narrow")
    blended = momentum + gradient.astype(jnp.float32)
    basis = lax.all_gather(right_factor, "wide", axis=0, tiled=True)
    projected = lax.psum(contract(blended, basis, ((1,), (1,)), HIGH), "narrow")
    gram = sum_over(contract(projected, projected, ((0,), (0,)), HIGH), "wide")
    sums = lax.psum_scatter(contract(blended, projected, ((0,), (0,)), HIGH), "wide", scatter_dimension=0, tiled=True)
    inverse = inverse_factor(gram)
    piece = contract(sums, inverse, ((1,), (1,)), HIGHEST)
    left = contract(projected, inverse, ((1,), (1,)), HIGH)
    squares = jnp.broadcast_to(jnp.sum(piece * piece, axis=0)[None, :], (8, piece.shape[1]))
    squares = sum_over(sum_over(squares, "wide"), "narrow")[0]
    root_mean = jnp.sqrt(squares / columns + EPS)
    right = lax.all_gather(piece, "wide", axis=0, tiled=True)
    own = lax.axis_index("wide") * right_factor.shape[0]
    count = right_factor.shape[0]
    new_right = lax.dynamic_slice_in_dim(right, own, count, 1).T / lax.dynamic_slice_in_dim(root_mean, own, count, 0)[:, None]
    feedback = contract(left, right, ((1,), (1,)), lax.Precision.DEFAULT)
    new_momentum = blended - (1.0 - MU) * feedback
    direction = contract(left / root_mean[None, :], right, ((1,), (1,)), HIGH)
    return new_momentum, new_right, direction.astype(jnp.bfloat16)


def solution(mesh):
    spec = P("wide", "narrow")
    return jax.shard_map(
        per_device,
        mesh=mesh,
        in_specs=(spec, spec, spec),
        out_specs=(spec, spec, spec),
        check_vma=False,
    )
```

time: 574 us -> 322 us (0.56); the launches traced: 566 us -> 322 us
  other arithmetic: 128 us -> 3.29 us
  waiting for transfers between devices: 260 us -> 203 us
  matrix products: 118 us -> 63.2 us
  blocking collectives: 23.8 us -> 0 us
  Pallas kernels: 0 us -> 22.8 us
  local copies, waits for them, and re-layouts: 17.7 us -> 2.73 us
  starting transfers between devices: 0.41 us -> 12.5 us
    another operation x17 -> x0, other arithmetic: 125 us -> none  [the longest x14 83.1 us: orthonormal(): factor_lower = jnp.linalg.cholesky(gram_matrix)]
    psum x2 -> x1, waiting for transfers between devices: 150 us -> 94.7 us  [per_device(): projected = lax.psum(contract(blended, basis, ((1,), (1,)), HIGH), 'narrow')]
    reduce_scatter x1, waiting for transfers between devices: 53.1 us -> 0.01 us  [per_device(): lax.psum_scatter(contract(blended, projected, ((0,), (0,)), HIGH), 'wide'...]
    ppermute x0 -> x10, waiting for transfers between devices: none -> 45.9 us  [exchange_sum(): return x + lax.ppermute(x, axis, [(i, i ^ bit) for i in range(size)])]
    dot_general x5 -> x7, matrix products: 98.4 us -> 63.2 us  [contract(): lax.dot_general(left, right, (dims, ((), ())), preferred_element_type=jnp...]
    pallas_call x0 -> x1, Pallas kernels: none -> 22.8 us  [inverse_factor(): pl.pallas_call(factor_kernel, out_shape=jax.ShapeDtypeStruct(gram.shape,...]
    another operation x13 -> x0, matrix products: 19.9 us -> none  [the longest x7 13.5 us: orthonormal(): jax.scipy.linalg.solve_triangular(factor_lower, projected.T, lower=True)]
    another operation x17 -> x0, local copies, waits for them, and re-layouts: 14.4 us -> none
  transfers between devices with their start and end apart: 5 -> 14, of which waited for: 5 -> 11; matrix products, arithmetic and copies ran while one was open for 1% -> 3% of each run, Pallas kernels for 0% -> 7%
where the time goes in v1:
time: 322 us
  waiting for transfers between devices  203 us (63%)
  matrix products  63.2 us (20%)
  Pallas kernels  22.8 us (7%)
  between operations  13.8 us (4%)
  starting transfers between devices  12.5 us (4%)
  other arithmetic  3.29 us (1%)
    psum x1, waiting for transfers between devices, per_device(): projected = lax.psum(contract(blended, basis, ((1,), (1,)), HIGH), 'narrow')  94.7 us
    dot_general x7, matrix products, contract(): lax.dot_general(left, right, (dims, ((), ())), preferred_element_type=jnp...  63.2 us
    ppermute x10, waiting for transfers between devices, exchange_sum(): return x + lax.ppermute(x, axis, [(i, i ^ bit) for i in range(size)])  45.9 us
    all_gather x1, waiting for transfers between devices, per_device(): basis = lax.all_gather(right_factor, 'wide', axis=0, tiled=True)  43.5 us
    pallas_call x1, Pallas kernels, inverse_factor(): pl.pallas_call(factor_kernel, out_shape=jax.ShapeDtypeStruct(gram.shape,...  22.8 us
    all_gather x1, waiting for transfers between devices, per_device(): right = lax.all_gather(piece, 'wide', axis=0, tiled=True)  18.3 us
    ppermute x10, starting transfers between devices, exchange_sum(): return x + lax.ppermute(x, axis, [(i, i ^ bit) for i in range(size)])  12.2 us
  transfers between devices with their start and end apart: 14, of which 11 were waited for; matrix products, arithmetic and copies ran while one was open for 3% of the time, Pallas kernels for 7%

profile of v1, /device:TPU:0, one launch (start us, length us, event | category | flops | bytes accessed | tf_op | source)
XLA Modules:
  0.0 321.5 jit_solution(13964859005786564155)
XLA Ops:
  7.2 0.0 all-gather.3.cloned.1.call-start
  7.2 0.7 all-gather.3.cloned.1.call-update
  7.9 0.0 all-reduce.2.cloned.1.call-start
  7.9 43.5 %all-gather.3.cloned.1.call-done = f32[512,2304]{1,0:T(8,128)} async-done(((f32[64,2304]{1,0:T(8,128)}), f32[512,2304]{1,0:T(8,128)}) %all-gather.3.cloned.1.call-update) | async-done | bytes 4718608 | tf_op jit(solution)/shard_map/all_gather | solution.py:139
  51.4 14.3 %fusion.2 = f32[1152,512]{1,0:T(8,128)} fusion(f32[512,2304]{1,0:T(8,128)} %all-gather.3.cloned.1.call-done, f32[1152,2304]{1,0:T(8,128)} %param.3, bf16[1152,2304]{1,0:T(8,128)(2,1)} %param.4), kind=kOutput, calls=%fused_computation.5 | convolution fusion | flops 8159035392 | bytes 23003136 | tf_op jit(solution)/shard_map/dot_general | solution.py:105
  65.7 0.0 all-reduce.2.cloned.1.call-update
  65.8 0.0 reduce-scatter.2.cloned.1.call-start
  65.8 94.7 %all-reduce.2.cloned.1.call-done = f32[1152,512]{1,0:T(8,128)} async-done(((f32[1152,512]{1,0:T(8,128)}), f32[1152,512]{1,0:T(8,128)}) %all-reduce.2.cloned.1.call-update) | async-done | bytes 2359312 | tf_op jit(solution)/shard_map/psum | solution.py:140
  160.5 15.0 %fusion.1 = f32[2304,512]{1,0:T(8,128)} fusion(f32[1152,512]{1,0:T(8,128)} %all-reduce.2.cloned.1.call-done, f32[1152,2304]{1,0:T(8,128)} %param.3, bf16[1152,2304]{1,0:T(8,128)(2,1)} %param.4), kind=kOutput, calls=%fused_computation.4 | convolution fusion | flops 8159035392 | bytes 23003136 | tf_op jit(solution)/shard_map/dot_general | solution.py:105
  175.6 0.0 reduce-scatter.2.cloned.1.call-update
  175.6 0.2 all-gather.5.cloned.1.call-start
  175.8 1.4 copy-done
  177.2 2.2 fusion.7
  179.5 0.1 collective-permute-start
  179.6 3.5 %collective-permute-done = f32[512,512]{1,0:T(8,128)S(1)} collective-permute-done((f32[512,512]{1,0:T(8,128)S(1)}, f32[512,512]{1,0:T(8,128)S(1)}, u32[]{:S(2)}, u32[]{:S(2)}) %collective-permute-start) | collective-permute-done | bytes 1048608 | tf_op jit(solution)/shard_map/ppermute | solution.py:110
  183.0 0.2 add.50
  183.3 0.1 fusion.6
  183.3 1.6 collective-permute-start.1
  184.9 1.5 collective-permute-start.3
  186.4 11.0 %collective-permute-done.1 = f32[256,512]{1,0:T(8,128)S(1)} collective-permute-done((f32[256,512]{1,0:T(8,128)S(1)}, f32[256,512]{1,0:T(8,128)S(1)}, u32[]{:S(2)}, u32[]{:S(2)}) %collective-permute-start.1) | collective-permute-done | bytes 524320 | tf_op jit(solution)/shard_map/ppermute | solution.py:110
  197.4 1.4 collective-permute-done.3
  198.8 0.2 slice_add_fusion.2
  199.0 2.5 collective-permute-start.2
  201.5 0.0 collective-permute-start.4
  201.5 21.8 %collective-permute-done.2 = f32[256,512]{1,0:T(8,128)S(1)} collective-permute-done((f32[256,512]{1,0:T(8,128)S(1)}, f32[256,512]{1,0:T(8,128)S(1)}, u32[]{:S(2)}, u32[]{:S(2)}) %collective-permute-start.2) | collective-permute-done | bytes 524320 | tf_op jit(solution)/shard_map/ppermute | solution.py:110
  223.3 0.1 add.52
  223.4 0.0 collective-permute-done.4
  223.4 0.1 add.54
  223.5 1.0 pad_maximum_fusion.gram_ref
  224.5 22.8 %inverse_factor.1 = f32[512,512]{1,0:T(8,128)} custom-call(f32[512,512]{1,0:T(8,128)} %pad_maximum_fusion.gram_ref), custom_call_target="tpu_custom_call" | custom-call | flops 8589934592 | bytes 2097152 | tf_op jit(solution)/shard_map/inverse_factor/pallas_call | solution.py:99
  247.3 3.4 %multiply_reduce_fusion = (f32[512]{0:T(512)S(1)}, f32[288,512]{1,0:T(8,128)}) fusion(f32[288,512]{1,0:T(8,128)} %reduce-scatter.2.cloned.1.call-done, f32[512,512]{1,0:T(8,128)} %inverse_factor.1), kind=kOutput, calls=%fused_computation.10 | convolution fusion | flops 906264064 | bytes 2230272 | tf_op jit(solution)/shard_map/dot_general | solution.py:105
  250.7 0.0 all-gather.5.cloned.1.call-update
  250.7 0.1 collective-permute-start.5
  250.8 1.2 collective-permute-done.5
  251.9 1.4 collective-permute-start.6
  253.3 2.4 collective-permute-done.6
  255.7 1.4 collective-permute-start.7
  257.1 2.4 collective-permute-done.7
  259.4 1.4 collective-permute-start.8
  260.8 2.3 collective-permute-done.8
  263.2 2.3 collective-permute-start.9
  265.5 4.7 %fusion.8 = f32[1152,512]{1,0:T(8,128)} fusion(f32[1152,512]{1,0:T(8,128)S(1)} %copy-done, f32[512,512]{1,0:T(8,128)} %inverse_factor.1), kind=kOutput, calls=%fused_computation.20 | convolution fusion | flops 1811939328 | bytes 5767168 | tf_op jit(solution)/shard_map/dot_general | solution.py:105
  270.2 0.1 dynamic-slice_bitcast_fusion
  270.3 18.3 %all-gather.5.cloned.1.call-done = f32[2304,512]{1,0:T(8,128)} async-done(((f32[288,512]{1,0:T(8,128)}), f32[2304,512]{1,0:T(8,128)}) %all-gather.5.cloned.1.call-update) | async-done | bytes 4718608 | tf_op jit(solution)/shard_map/all_gather | solution.py:149
  288.6 1.6 divide_bitcast_fusion
  290.3 1.2 copy.6
  291.4 10.9 %fusion = f32[1152,2304]{1,0:T(8,128)} fusion(f32[1152,512]{1,0:T(8,128)S(1)} %copy-done.1, f32[2304,512]{1,0:T(8,128)} %all-gather.5.cloned.1.call-done, f32[1152,2304]{1,0:T(8,128)} %param.3, bf16[1152,2304]{1,0:T(8,128)(2,1)} %param.4), kind=kOutput, calls=%fused_computation.1 | convolution fusion | flops 2728525824 | bytes 33619968 | tf_op jit(solution)/shard_map/dot_general | solution.py:105
  302.4 12.6 %convolution_convert_fusion = bf16[1152,2304]{1,0:T(8,128)(2,1)} fusion(f32[2304,512]{1,0:T(8,128)} %all-gather.5.cloned.1.call-done, f32[1152,512]{1,0:T(8,128)S(1)} %copy-done.1, f32[512]{0:T(512)S(1)} %bitcast.16), kind=kOutput, calls=%fused_computation.2 | convolution fusion | flops 8156971008 | bytes 12388352 | tf_op jit(solution)/shard_map/dot_general | solution.py:105
  (11 shorter events, 0.0 us)
Async XLA Ops:
  7.2 44.2 %all-gather.3.cloned.1.call-start = ((), (), s32[]{:S(2)}) async-start(), calls=%async_computation.1 | async-start | bytes 5308416 | tf_op jit(solution)/shard_map/all_gather | solution.py:139
  7.9 152.6 %all-reduce.2.cloned.1.call-start = ((), (), s32[]{:S(2)}) async-start(), calls=%async_computation.2 | async-start | bytes 4718592 | tf_op jit(solution)/shard_map/psum | solution.py:140
  65.8 181.5 %reduce-scatter.2.cloned.1.call-start = ((), (), s32[]{:S(2)}) async-start(), calls=%async_computation.3 | async-start | bytes 5308416 | tf_op jit(solution)/shard_map/reduce_scatter | solution.py:142
  175.6 1.7 copy-start
  175.6 113.0 %all-gather.5.cloned.1.call-start = ((), (), s32[]{:S(2)}) async-start(), calls=%async_computation.4 | async-start | bytes 5308416 | tf_op jit(solution)/shard_map/all_gather | solution.py:149
  179.5 3.5 %collective-permute-start = (f32[512,512]{1,0:T(8,128)S(1)}, f32[512,512]{1,0:T(8,128)S(1)}, u32[]{:S(2)}, u32[]{:S(2)}) collective-permute-start(f32[512,512]{1,0:T(8,128)S(1)} %fusion.7), channel_id=1, source_target_pairs={{0,4},{4,0},{8,12},{12,8},{16,20},{20,16},{24,28},{28,24},{1,5},{5... | collective-permute-start | bytes 3145736 | tf_op jit(solution)/shard_map/ppermute | solution.py:110
  183.3 14.1 %collective-permute-start.1 = (f32[256,512]{1,0:T(8,128)S(1)}, f32[256,512]{1,0:T(8,128)S(1)}, u32[]{:S(2)}, u32[]{:S(2)}) collective-permute-start(f32[256,512]{1,0:T(8,128)S(1)} %get-tuple-element.8), channel_id=1, source_target_pairs={{0,8},{4,12},{8,0},{12,4},{16,24},{20,28},{24,16},{28,20},{1,9},{5... | collective-permute-start | bytes 1572872 | tf_op jit(solution)/shard_map/ppermute | solution.py:110
  184.9 13.9 %collective-permute-start.3 = (f32[256,512]{1,0:T(8,128)S(1)}, f32[256,512]{1,0:T(8,128)S(1)}, u32[]{:S(2)}, u32[]{:S(2)}) collective-permute-start(f32[256,512]{1,0:T(8,128)S(1)} %get-tuple-element.9), channel_id=1, source_target_pairs={{0,16},{4,20},{8,24},{12,28},{16,0},{20,4},{24,8},{28,12},{1,17},{... | collective-permute-start | bytes 1572872 | tf_op jit(solution)/shard_map/ppermute | solution.py:110
  199.0 24.3 %collective-permute-start.2 = (f32[256,512]{1,0:T(8,128)S(1)}, f32[256,512]{1,0:T(8,128)S(1)}, u32[]{:S(2)}, u32[]{:S(2)}) collective-permute-start(f32[256,512]{1,0:T(8,128)S(1)} %get-tuple-element.6), channel_id=1, source_target_pairs={{0,16},{4,20},{8,24},{12,28},{16,0},{20,4},{24,8},{28,12},{1,17},{... | collective-permute-start | bytes 1572872 | tf_op jit(solution)/shard_map/ppermute | solution.py:110
  201.5 21.9 %collective-permute-start.4 = (f32[256,512]{1,0:T(8,128)S(1)}, f32[256,512]{1,0:T(8,128)S(1)}, u32[]{:S(2)}, u32[]{:S(2)}) collective-permute-start(f32[256,512]{1,0:T(8,128)S(1)} %get-tuple-element.7), channel_id=1, source_target_pairs={{0,8},{4,12},{8,0},{12,4},{16,24},{20,28},{24,16},{28,20},{1,9},{5... | collective-permute-start | bytes 1572872 | tf_op jit(solution)/shard_map/ppermute | solution.py:110
  250.7 1.2 collective-permute-start.5
  251.9 3.7 %collective-permute-start.6 = (f32[8,512]{1,0:T(8,128)S(1)}, f32[8,512]{1,0:T(8,128)S(1)}, u32[]{:S(2)}, u32[]{:S(2)}) collective-permute-start(f32[8,512]{1,0:T(8,128)S(1)} %broadcast_add_fusion), channel_id=1, source_target_pairs={{0,8},{4,12},{8,0},{12,4},{16,24},{20,28},{24,16},{28,20},{1,9},{5... | collective-permute-start | bytes 49160 | tf_op jit(solution)/shard_map/ppermute | solution.py:110
  255.7 3.7 %collective-permute-start.7 = (f32[8,512]{1,0:T(8,128)S(1)}, f32[8,512]{1,0:T(8,128)S(1)}, u32[]{:S(2)}, u32[]{:S(2)}) collective-permute-start(f32[8,512]{1,0:T(8,128)S(1)} %fusion.20), channel_id=1, source_target_pairs={{0,16},{4,20},{8,24},{12,28},{16,0},{20,4},{24,8},{28,12},{1,17},{... | collective-permute-start | bytes 49160 | tf_op jit(solution)/shard_map/ppermute | solution.py:110
  259.4 3.7 %collective-permute-start.8 = (f32[8,512]{1,0:T(8,128)S(1)}, f32[8,512]{1,0:T(8,128)S(1)}, u32[]{:S(2)}, u32[]{:S(2)}) collective-permute-start(f32[8,512]{1,0:T(8,128)S(1)} %add.58), channel_id=1, source_target_pairs={{0,1},{1,0},{2,3},{3,2},{4,5},{5,4},{6,7},{7,6},{8,9},{9,8},{10,11... | collective-permute-start | bytes 49160 | tf_op jit(solution)/shard_map/ppermute | solution.py:110
  263.2 7.0 %collective-permute-start.9 = (f32[8,512]{1,0:T(8,128)S(1)}, f32[8,512]{1,0:T(8,128)S(1)}, u32[]{:S(2)}, u32[]{:S(2)}) collective-permute-start(f32[8,512]{1,0:T(8,128)S(1)} %add.59), channel_id=1, source_target_pairs={{0,2},{1,3},{2,0},{3,1},{4,6},{5,7},{6,4},{7,5},{8,10},{9,11},{10,... | collective-permute-start | bytes 49160 | tf_op jit(solution)/shard_map/ppermute | solution.py:110
  270.2 21.3 %copy-start.1 = (f32[1152,512]{1,0:T(8,128)S(1)}, f32[1152,512]{1,0:T(8,128)}, u32[]{:S(2)}) copy-start(f32[1152,512]{1,0:T(8,128)} %fusion.8) | copy-start | bytes 7077892
Sparse Core Ops, SparseCore 0:
  9.9 41.4 all-gather.2
  65.9 94.6 all-reduce.1
  175.7 63.1 reduce-scatter.1
  250.8 37.7 all-gather.4
